TPU v7x, 32 devices: a whole 2x2x4 slice. The times are simulated.
32 devices in a mesh: gx: 4 (over z), gy: 4 (over y, core), gz: 2 (over x).
Axes of the slice: x: 2, y: 2, z: 4, core: 2. Of those that a mesh axis runs over, the one named last changes fastest.
Arguments:
- gas_position: float32 [3, 131072], P(None, ('gx', 'gy', 'gz')), may hold values from 0 to 1
- gas_mass: float32 [131072], P(('gx', 'gy', 'gz')), may hold values from 0.3 to 3
- gas_smoothing: float32 [131072], P(('gx', 'gy', 'gz')), may hold values from 0.5 to 1.5
- leaf_counts: int32 [1024], P(('gx', 'gy', 'gz')), may hold values from 64 to 128
- ghost_lists: int32 [32, 4, 2], P(('gx', 'gy', 'gz')), may hold values from 0 to 31, as said below
- star_position: float32 [3, 65536], P(None, ('gx', 'gy', 'gz')), may hold values from 0 to 1
- star_energy: float32 [65536], P(('gx', 'gy', 'gz')), may hold values from 0.1 to 10
- star_momentum: float32 [3, 65536], P(None, ('gx', 'gy', 'gz')), may hold values from -6 to 6
- block_counts: int32 [512], P(('gx', 'gy', 'gz')), may hold values from 1 to 128
- block_owners: int32 [512, 1], P(('gx', 'gy', 'gz')), may hold values from 0 to 7; in each aligned block of 16 rows (0 to 15, 16 to 31, ...) at most 3 rows name the same one
- block_leaves: int32 [512], P(('gx', 'gy', 'gz')), may hold values from 0 to 31
Outputs:
- accel: float32 [3, 131072], P(None, ('gx', 'gy', 'gz'))
- deposit: float32 [4, 131072], P(None, ('gx', 'gy', 'gz'))
Inputs may be any that keep to these rules, and one draw needn't show every extreme that they name: `ghost_lists`: each of the four lists of a device names 2 different leaves. `block_owners`: among the 16 star blocks of one device, no owner is named more than 3 times, and in some devices one owner is named exactly 3 times.
All inputs are finite; a program needn't handle non-finite values.
Results may differ from a plain program's by a relative error of at most 0.00015.
Values sent between devices are 32-bit elements; how exact they have to be, the bound alone decides.
A program may use at most 64 MiB of HBM per device.

v0:
```python
import jax
import jax.numpy as jnp
from jax import lax
from jax.sharding import PartitionSpec as P

LEAVES = 32
LEAF_SLOTS = 128
STARS_BLOCK = 128
SLOTS = 3


SPLIT_SQ = 1.0
SOFT_SQ = 0.01
GRAVITY = 0.002
RADIAL_PUSH = 1.0


def from_behind(shard, axis, by):
    size = lax.axis_size(axis)
    return lax.ppermute(shard, axis, [(i, (i + by) % size) for i in range(size)])


def pair_accel(targets, sources, source_mass):
    sep_x = sources[0][None, :] - targets[0][:, None]
    sep_y = sources[1][None, :] - targets[1][:, None]
    sep_z = sources[2][None, :] - targets[2][:, None]
    distance = sep_x * sep_x + sep_y * sep_y + sep_z * sep_z
    soften = distance + SOFT_SQ
    kernel = source_mass[None, :] * jnp.exp(-distance / SPLIT_SQ) / (soften * jnp.sqrt(soften))
    return GRAVITY * jnp.stack(
        [
            jnp.sum(sep_x * kernel, axis=1),
            jnp.sum(sep_y * kernel, axis=1),
            jnp.sum(sep_z * kernel, axis=1),
        ]
    )


def deposit_block(star_xyz, energy_in, momentum_in, gas_xyz, inverse):
    seps = [gas_xyz[axis_num][None, :] - star_xyz[axis_num][:, None] for axis_num in range(3)]
    distance = seps[0] * seps[0] + seps[1] * seps[1] + seps[2] * seps[2]
    weight = jnp.exp(-distance * inverse[None, :])
    normaliser = 1.0 + jnp.sum(weight, axis=1)
    shares = weight / normaliser[:, None]
    heated = jnp.sum(energy_in[:, None] * shares, axis=0)
    kicks = [
        jnp.sum(
            shares
            * (momentum_in[axis_num][:, None] + RADIAL_PUSH * energy_in[:, None] * seps[axis_num]),
            axis=0,
        )
        for axis_num in range(3)
    ]
    return jnp.stack([heated] + kicks)


def gather_ghosts(carried, leaf_lists):
    arrivals = []
    for which, shift_by, offset in ((0, 1, -1.0), (1, -1, 1.0)):
        outbound = carried[:, leaf_lists[which], :].reshape(4, -1)
        arrived = from_behind(outbound, "gx", shift_by)
        arrivals.append(arrived.at[0].add(offset))
    for which, shift_by, offset in ((2, 1, -1.0), (3, -1, 1.0)):
        outbound = carried[:, leaf_lists[which], :].reshape(4, -1)
        arrived = from_behind(outbound, "gy", shift_by)
        arrivals.append(arrived.at[1].add(offset))
    return arrivals


def owner_work(received, gas_table):
    lead, items = (received.shape[0], received.shape[1])
    flattened = received.reshape(lead * items, 8, STARS_BLOCK)
    marker = flattened[:, 7, :LEAVES]
    gathered = jnp.dot(
        marker, gas_table, precision=lax.Precision.HIGHEST, preferred_element_type=jnp.float32
    ).reshape(lead * items, 4, LEAF_SLOTS)
    deposits = lax.map(
        lambda pair_items: deposit_block(
            pair_items[0][:3],
            pair_items[0][3],
            pair_items[0][4:7],
            pair_items[1][:3],
            pair_items[1][3],
        ),
        (flattened, gathered),
        batch_size=16,
    )
    return (deposits.reshape(lead, items, 4, LEAF_SLOTS), marker.reshape(lead, items, LEAVES))


def on_device(
    gas_position,
    gas_mass,
    gas_smoothing,
    leaf_counts,
    ghost_lists,
    star_position,
    star_energy,
    star_momentum,
    block_counts,
    block_owners,
    block_leaves,
):
    rows = LEAVES * LEAF_SLOTS
    blocks_here = block_counts.shape[0]
    alive = (jnp.arange(LEAF_SLOTS, dtype=jnp.int32)[None, :] < leaf_counts[:, None]).reshape(rows)
    masses = jnp.where(alive, gas_mass, jnp.float32(0.0))
    carried = jnp.concatenate([gas_position, masses[None]], axis=0).reshape(4, LEAVES, LEAF_SLOTS)
    star_live = jnp.arange(STARS_BLOCK, dtype=jnp.int32)[None, :] < block_counts[:, None]
    star_xyz = star_position.reshape(3, blocks_here, STARS_BLOCK).transpose(1, 0, 2)
    energy_in = jnp.where(
        star_live, star_energy.reshape(blocks_here, STARS_BLOCK), jnp.float32(0.0)
    )
    momentum_in = jnp.where(
        star_live[:, None, :],
        star_momentum.reshape(3, blocks_here, STARS_BLOCK).transpose(1, 0, 2),
        jnp.float32(0.0),
    )
    marker_rows = (
        jnp.arange(STARS_BLOCK, dtype=jnp.int32)[None, :] == block_leaves[:, None]
    ).astype(jnp.float32)
    payload = jnp.concatenate(
        [star_xyz, energy_in[:, None, :], momentum_in, marker_rows[:, None, :]], axis=1
    )
    group_y = lax.axis_size("gy")
    group_z = lax.axis_size("gz")
    owners = group_y * group_z
    owner_ids = block_owners[:, 0]
    matches = (owner_ids[:, None] == jnp.arange(owners, dtype=jnp.int32)[None, :]).astype(jnp.int32)
    earlier = jnp.cumsum(matches, axis=0) - matches
    position_rank = jnp.sum(earlier * matches, axis=1)
    slot_index = owner_ids * SLOTS + position_rank
    placing = (jnp.arange(owners * SLOTS, dtype=jnp.int32)[:, None] == slot_index[None, :]).astype(
        jnp.float32
    )
    outgoing = jnp.dot(
        placing,
        payload.reshape(blocks_here, 8 * STARS_BLOCK),
        precision=lax.Precision.HIGHEST,
        preferred_element_type=jnp.float32,
    ).reshape(owners, SLOTS, 8, STARS_BLOCK)
    inverse = 1.0 / (gas_smoothing * gas_smoothing)
    gas_table = (
        jnp.concatenate(
            [gas_position.reshape(3, LEAVES, LEAF_SLOTS), inverse.reshape(1, LEAVES, LEAF_SLOTS)],
            axis=0,
        )
        .transpose(1, 0, 2)
        .reshape(LEAVES, 4 * LEAF_SLOTS)
    )
    deposits, markers = owner_work(
        lax.all_to_all(outgoing, ("gy", "gz"), split_axis=0, concat_axis=0, tiled=True), gas_table
    )
    arrivals = gather_ghosts(carried, ghost_lists[0])
    sources = jnp.concatenate([carried.reshape(4, rows)] + arrivals, axis=1)
    per_turn = max(1, LEAVES // 16) * LEAF_SLOTS
    turns = rows // per_turn
    targets = gas_position.reshape(3, turns, per_turn).transpose(1, 0, 2)
    accel_blocks = lax.map(
        lambda block_targets: pair_accel(block_targets, sources[:3], sources[3]), targets
    )
    accel = jnp.where(
        alive[None, :], accel_blocks.transpose(1, 0, 2).reshape(3, rows), jnp.float32(0.0)
    )
    slot_total = owners * SLOTS
    summed = jnp.dot(
        markers.reshape(slot_total, LEAVES).T,
        deposits.reshape(slot_total, 4 * LEAF_SLOTS),
        precision=lax.Precision.HIGHEST,
        preferred_element_type=jnp.float32,
    )
    summed = summed.reshape(LEAVES, 4, LEAF_SLOTS).transpose(1, 0, 2).reshape(4, rows)
    deposit = jnp.where(alive[None, :], summed, jnp.float32(0.0))
    return (accel, deposit)


def solution(mesh):
    placed = (
        P(None, ("gx", "gy", "gz")),
        P(("gx", "gy", "gz")),
        P(("gx", "gy", "gz")),
        P(("gx", "gy", "gz")),
        P(("gx", "gy", "gz"), None, None),
        P(None, ("gx", "gy", "gz")),
        P(("gx", "gy", "gz")),
        P(None, ("gx", "gy", "gz")),
        P(("gx", "gy", "gz")),
        P(("gx", "gy", "gz"), None),
        P(("gx", "gy", "gz")),
    )
    return jax.shard_map(
        on_device,
        mesh=mesh,
        in_specs=placed,
        out_specs=(P(None, ("gx", "gy", "gz")), P(None, ("gx", "gy", "gz"))),
        check_vma=False,
    )
```

profile of v0, /device:TPU:0, one launch (start us, length us, event | category | flops | bytes accessed | tf_op | source)
XLA Modules:
  0.0 131.7 jit_solution(13442771296206850068)
XLA Ops:
  0.6 0.8 multiply_divide_fusion
  1.4 1.0 slice_reduce_fusion
  2.5 0.8 broadcast_select_fusion.1
  3.9 3.1 %collective-permute-start = (f32[4,256]{1,0:T(4,128)S(1)}, f32[4,256]{1,0:T(4,128)S(1)}, u32[]{:S(2)}, u32[]{:S(2)}) collective-permute-start(f32[4,256]{1,0:T(4,128)S(1)} %bitcast.236), channel_id=1, source_target_pairs={{0,8},{8,16},{16,24},{24,0},{1,9},{9,17},{17,25},{25,1},{2,10},{10... | collective-permute-start | bytes 12296 | tf_op jit(solution)/shard_map/ppermute | solution.py:20
  7.6 2.1 %collective-permute-start.1 = (f32[4,256]{1,0:T(4,128)S(1)}, f32[4,256]{1,0:T(4,128)S(1)}, u32[]{:S(2)}, u32[]{:S(2)}) collective-permute-start(f32[4,256]{1,0:T(4,128)S(1)} %bitcast.234), channel_id=1, source_target_pairs={{0,24},{8,0},{16,8},{24,16},{1,25},{9,1},{17,9},{25,17},{2,26},{10... | collective-permute-start | bytes 12296 | tf_op jit(solution)/shard_map/ppermute | solution.py:20
  10.9 1.8 %collective-permute-start.3 = (f32[4,256]{1,0:T(4,128)S(1)}, f32[4,256]{1,0:T(4,128)S(1)}, u32[]{:S(2)}, u32[]{:S(2)}) collective-permute-start(f32[4,256]{1,0:T(4,128)S(1)} %bitcast.235), channel_id=1, source_target_pairs={{0,6},{2,0},{4,2},{6,4},{1,7},{3,1},{5,3},{7,5},{8,14},{10,8},{12,... | collective-permute-start | bytes 12296 | tf_op jit(solution)/shard_map/ppermute | solution.py:20
  13.6 0.6 copy.32
  14.3 3.9 %all-to-all-start = ((f32[8,3,8,128]{3,2,1,0:T(8,128)}), f32[8,3,8,128]{3,2,1,0:T(8,128)S(1)}, u32[]{:S(2)}, u32[]{:S(2)}) async-start(f32[8,3,8,128]{3,2,1,0:T(8,128)} %copy.32), calls=%async_computation | async-start | bytes 196608 | tf_op jit(solution)/shard_map/all_to_all | solution.py:152
  18.2 0.6 copy-done.5
  19.2 104.0 %while.18 = (s32[]{:T(128)}, f32[16,3,256]{2,1,0:T(4,128)S(1)}, f32[4,5120]{1,0:T(4,128)S(1)}, f32[16,3,256]{2,1,0:T(4,128)S(1)}, s32[]{:T(128)}, /*index=5*/s32[]{:T(128)}, s32[]{}, s32[]{}) while((s32[]{:T(128)}, f32[16,3,256]{2,1,0:T(4,128)S(1)}, f32[4,5120]{1,0:T(4,128)S(1)}, f32[16,3,256]{2,1,0:T(4,128)S(1)}, s32[]{:T(128)}, ...), condition=%wide.region_4.5_spmd, body=%wide.region_0.0_spmd.sunk | while | flops 24905220 | bytes 265349 | solution.py:159
  19.3 6.4 %fusion.71 = (f32[256]{0:T(256)S(1)}, f32[256]{0:T(256)S(1)}, f32[256]{0:T(256)S(1)}) fusion(f32[256]{0:T(256)S(1)} %bitcast.196, f32[5120]{0:T(1024)S(1)} %bitcast.180, f32[256]{0:T(256)S(1)} %bitcast.197, f32[5120]{0:T(1024)S(1)} %bitcast.178, f32[256]{0:T(256)S(1)} %bitcast.195, f32[5120]{0:T(1024)S(1)} %bitcast.179, f32[5120]{0:T(1024)S(1)} %bitcast.177), kind=kLoop, calls=%fused_computation.13.clone.1 | loop fusion | flops 24902912 | bytes 88064 | tf_op jit(solution)/shard_map/while/body/eval_jaxpr/reduce_sum | solution.py:32
  25.8 6.4 %fusion.71 = (f32[256]{0:T(256)S(1)}, f32[256]{0:T(256)S(1)}, f32[256]{0:T(256)S(1)}) fusion(f32[256]{0:T(256)S(1)} %bitcast.196, f32[5120]{0:T(1024)S(1)} %bitcast.180, f32[256]{0:T(256)S(1)} %bitcast.197, f32[5120]{0:T(1024)S(1)} %bitcast.178, f32[256]{0:T(256)S(1)} %bitcast.195, f32[5120]{0:T(1024)S(1)} %bitcast.179, f32[5120]{0:T(1024)S(1)} %bitcast.177), kind=kLoop, calls=%fused_computation.13.clone.1 | loop fusion | flops 24902912 | bytes 88064 | tf_op jit(solution)/shard_map/while/body/eval_jaxpr/reduce_sum | solution.py:32
  32.3 6.4 %fusion.71 = (f32[256]{0:T(256)S(1)}, f32[256]{0:T(256)S(1)}, f32[256]{0:T(256)S(1)}) fusion(f32[256]{0:T(256)S(1)} %bitcast.196, f32[5120]{0:T(1024)S(1)} %bitcast.180, f32[256]{0:T(256)S(1)} %bitcast.197, f32[5120]{0:T(1024)S(1)} %bitcast.178, f32[256]{0:T(256)S(1)} %bitcast.195, f32[5120]{0:T(1024)S(1)} %bitcast.179, f32[5120]{0:T(1024)S(1)} %bitcast.177), kind=kLoop, calls=%fused_computation.13.clone.1 | loop fusion | flops 24902912 | bytes 88064 | tf_op jit(solution)/shard_map/while/body/eval_jaxpr/reduce_sum | solution.py:32
  38.8 6.4 %fusion.71 = (f32[256]{0:T(256)S(1)}, f32[256]{0:T(256)S(1)}, f32[256]{0:T(256)S(1)}) fusion(f32[256]{0:T(256)S(1)} %bitcast.196, f32[5120]{0:T(1024)S(1)} %bitcast.180, f32[256]{0:T(256)S(1)} %bitcast.197, f32[5120]{0:T(1024)S(1)} %bitcast.178, f32[256]{0:T(256)S(1)} %bitcast.195, f32[5120]{0:T(1024)S(1)} %bitcast.179, f32[5120]{0:T(1024)S(1)} %bitcast.177), kind=kLoop, calls=%fused_computation.13.clone.1 | loop fusion | flops 24902912 | bytes 88064 | tf_op jit(solution)/shard_map/while/body/eval_jaxpr/reduce_sum | solution.py:32
  45.3 6.4 %fusion.71 = (f32[256]{0:T(256)S(1)}, f32[256]{0:T(256)S(1)}, f32[256]{0:T(256)S(1)}) fusion(f32[256]{0:T(256)S(1)} %bitcast.196, f32[5120]{0:T(1024)S(1)} %bitcast.180, f32[256]{0:T(256)S(1)} %bitcast.197, f32[5120]{0:T(1024)S(1)} %bitcast.178, f32[256]{0:T(256)S(1)} %bitcast.195, f32[5120]{0:T(1024)S(1)} %bitcast.179, f32[5120]{0:T(1024)S(1)} %bitcast.177), kind=kLoop, calls=%fused_computation.13.clone.1 | loop fusion | flops 24902912 | bytes 88064 | tf_op jit(solution)/shard_map/while/body/eval_jaxpr/reduce_sum | solution.py:32
  51.8 6.4 %fusion.71 = (f32[256]{0:T(256)S(1)}, f32[256]{0:T(256)S(1)}, f32[256]{0:T(256)S(1)}) fusion(f32[256]{0:T(256)S(1)} %bitcast.196, f32[5120]{0:T(1024)S(1)} %bitcast.180, f32[256]{0:T(256)S(1)} %bitcast.197, f32[5120]{0:T(1024)S(1)} %bitcast.178, f32[256]{0:T(256)S(1)} %bitcast.195, f32[5120]{0:T(1024)S(1)} %bitcast.179, f32[5120]{0:T(1024)S(1)} %bitcast.177), kind=kLoop, calls=%fused_computation.13.clone.1 | loop fusion | flops 24902912 | bytes 88064 | tf_op jit(solution)/shard_map/while/body/eval_jaxpr/reduce_sum | solution.py:32
  58.3 6.4 %fusion.71 = (f32[256]{0:T(256)S(1)}, f32[256]{0:T(256)S(1)}, f32[256]{0:T(256)S(1)}) fusion(f32[256]{0:T(256)S(1)} %bitcast.196, f32[5120]{0:T(1024)S(1)} %bitcast.180, f32[256]{0:T(256)S(1)} %bitcast.197, f32[5120]{0:T(1024)S(1)} %bitcast.178, f32[256]{0:T(256)S(1)} %bitcast.195, f32[5120]{0:T(1024)S(1)} %bitcast.179, f32[5120]{0:T(1024)S(1)} %bitcast.177), kind=kLoop, calls=%fused_computation.13.clone.1 | loop fusion | flops 24902912 | bytes 88064 | tf_op jit(solution)/shard_map/while/body/eval_jaxpr/reduce_sum | solution.py:32
  64.8 6.4 %fusion.71 = (f32[256]{0:T(256)S(1)}, f32[256]{0:T(256)S(1)}, f32[256]{0:T(256)S(1)}) fusion(f32[256]{0:T(256)S(1)} %bitcast.196, f32[5120]{0:T(1024)S(1)} %bitcast.180, f32[256]{0:T(256)S(1)} %bitcast.197, f32[5120]{0:T(1024)S(1)} %bitcast.178, f32[256]{0:T(256)S(1)} %bitcast.195, f32[5120]{0:T(1024)S(1)} %bitcast.179, f32[5120]{0:T(1024)S(1)} %bitcast.177), kind=kLoop, calls=%fused_computation.13.clone.1 | loop fusion | flops 24902912 | bytes 88064 | tf_op jit(solution)/shard_map/while/body/eval_jaxpr/reduce_sum | solution.py:32
  71.3 6.4 %fusion.71 = (f32[256]{0:T(256)S(1)}, f32[256]{0:T(256)S(1)}, f32[256]{0:T(256)S(1)}) fusion(f32[256]{0:T(256)S(1)} %bitcast.196, f32[5120]{0:T(1024)S(1)} %bitcast.180, f32[256]{0:T(256)S(1)} %bitcast.197, f32[5120]{0:T(1024)S(1)} %bitcast.178, f32[256]{0:T(256)S(1)} %bitcast.195, f32[5120]{0:T(1024)S(1)} %bitcast.179, f32[5120]{0:T(1024)S(1)} %bitcast.177), kind=kLoop, calls=%fused_computation.13.clone.1 | loop fusion | flops 24902912 | bytes 88064 | tf_op jit(solution)/shard_map/while/body/eval_jaxpr/reduce_sum | solution.py:32
  77.8 6.4 %fusion.71 = (f32[256]{0:T(256)S(1)}, f32[256]{0:T(256)S(1)}, f32[256]{0:T(256)S(1)}) fusion(f32[256]{0:T(256)S(1)} %bitcast.196, f32[5120]{0:T(1024)S(1)} %bitcast.180, f32[256]{0:T(256)S(1)} %bitcast.197, f32[5120]{0:T(1024)S(1)} %bitcast.178, f32[256]{0:T(256)S(1)} %bitcast.195, f32[5120]{0:T(1024)S(1)} %bitcast.179, f32[5120]{0:T(1024)S(1)} %bitcast.177), kind=kLoop, calls=%fused_computation.13.clone.1 | loop fusion | flops 24902912 | bytes 88064 | tf_op jit(solution)/shard_map/while/body/eval_jaxpr/reduce_sum | solution.py:32
  84.3 6.4 %fusion.71 = (f32[256]{0:T(256)S(1)}, f32[256]{0:T(256)S(1)}, f32[256]{0:T(256)S(1)}) fusion(f32[256]{0:T(256)S(1)} %bitcast.196, f32[5120]{0:T(1024)S(1)} %bitcast.180, f32[256]{0:T(256)S(1)} %bitcast.197, f32[5120]{0:T(1024)S(1)} %bitcast.178, f32[256]{0:T(256)S(1)} %bitcast.195, f32[5120]{0:T(1024)S(1)} %bitcast.179, f32[5120]{0:T(1024)S(1)} %bitcast.177), kind=kLoop, calls=%fused_computation.13.clone.1 | loop fusion | flops 24902912 | bytes 88064 | tf_op jit(solution)/shard_map/while/body/eval_jaxpr/reduce_sum | solution.py:32
  90.8 6.4 %fusion.71 = (f32[256]{0:T(256)S(1)}, f32[256]{0:T(256)S(1)}, f32[256]{0:T(256)S(1)}) fusion(f32[256]{0:T(256)S(1)} %bitcast.196, f32[5120]{0:T(1024)S(1)} %bitcast.180, f32[256]{0:T(256)S(1)} %bitcast.197, f32[5120]{0:T(1024)S(1)} %bitcast.178, f32[256]{0:T(256)S(1)} %bitcast.195, f32[5120]{0:T(1024)S(1)} %bitcast.179, f32[5120]{0:T(1024)S(1)} %bitcast.177), kind=kLoop, calls=%fused_computation.13.clone.1 | loop fusion | flops 24902912 | bytes 88064 | tf_op jit(solution)/shard_map/while/body/eval_jaxpr/reduce_sum | solution.py:32
  97.3 6.4 %fusion.71 = (f32[256]{0:T(256)S(1)}, f32[256]{0:T(256)S(1)}, f32[256]{0:T(256)S(1)}) fusion(f32[256]{0:T(256)S(1)} %bitcast.196, f32[5120]{0:T(1024)S(1)} %bitcast.180, f32[256]{0:T(256)S(1)} %bitcast.197, f32[5120]{0:T(1024)S(1)} %bitcast.178, f32[256]{0:T(256)S(1)} %bitcast.195, f32[5120]{0:T(1024)S(1)} %bitcast.179, f32[5120]{0:T(1024)S(1)} %bitcast.177), kind=kLoop, calls=%fused_computation.13.clone.1 | loop fusion | flops 24902912 | bytes 88064 | tf_op jit(solution)/shard_map/while/body/eval_jaxpr/reduce_sum | solution.py:32
  103.8 6.4 %fusion.71 = (f32[256]{0:T(256)S(1)}, f32[256]{0:T(256)S(1)}, f32[256]{0:T(256)S(1)}) fusion(f32[256]{0:T(256)S(1)} %bitcast.196, f32[5120]{0:T(1024)S(1)} %bitcast.180, f32[256]{0:T(256)S(1)} %bitcast.197, f32[5120]{0:T(1024)S(1)} %bitcast.178, f32[256]{0:T(256)S(1)} %bitcast.195, f32[5120]{0:T(1024)S(1)} %bitcast.179, f32[5120]{0:T(1024)S(1)} %bitcast.177), kind=kLoop, calls=%fused_computation.13.clone.1 | loop fusion | flops 24902912 | bytes 88064 | tf_op jit(solution)/shard_map/while/body/eval_jaxpr/reduce_sum | solution.py:32
  110.3 6.4 %fusion.71 = (f32[256]{0:T(256)S(1)}, f32[256]{0:T(256)S(1)}, f32[256]{0:T(256)S(1)}) fusion(f32[256]{0:T(256)S(1)} %bitcast.196, f32[5120]{0:T(1024)S(1)} %bitcast.180, f32[256]{0:T(256)S(1)} %bitcast.197, f32[5120]{0:T(1024)S(1)} %bitcast.178, f32[256]{0:T(256)S(1)} %bitcast.195, f32[5120]{0:T(1024)S(1)} %bitcast.179, f32[5120]{0:T(1024)S(1)} %bitcast.177), kind=kLoop, calls=%fused_computation.13.clone.1 | loop fusion | flops 24902912 | bytes 88064 | tf_op jit(solution)/shard_map/while/body/eval_jaxpr/reduce_sum | solution.py:32
  116.8 6.4 %fusion.71 = (f32[256]{0:T(256)S(1)}, f32[256]{0:T(256)S(1)}, f32[256]{0:T(256)S(1)}) fusion(f32[256]{0:T(256)S(1)} %bitcast.196, f32[5120]{0:T(1024)S(1)} %bitcast.180, f32[256]{0:T(256)S(1)} %bitcast.197, f32[5120]{0:T(1024)S(1)} %bitcast.178, f32[256]{0:T(256)S(1)} %bitcast.195, f32[5120]{0:T(1024)S(1)} %bitcast.179, f32[5120]{0:T(1024)S(1)} %bitcast.177), kind=kLoop, calls=%fused_computation.13.clone.1 | loop fusion | flops 24902912 | bytes 88064 | tf_op jit(solution)/shard_map/while/body/eval_jaxpr/reduce_sum | solution.py:32
  123.2 0.7 broadcast_select_fusion
  124.7 0.6 fusion.42
  125.5 1.3 %fusion.26 = f32[16,128]{1,0:T(8,128)S(1)} fusion(f32[16,128]{1,0:T(8,128)S(1)} %bitcast.214, f32[16,128]{1,0:T(8,128)S(1)} %bitcast.204, f32[16,128]{1,0:T(8,128)S(1)} %bitcast.216, f32[16,128]{1,0:T(8,128)S(1)} %bitcast.206, f32[16,128]{1,0:T(8,128)S(1)} %bitcast.218, f32[16,128]{1,0:T(8,128)S(1)} %bitcast.208, f32[16,128]{1,0:T(8,128)S(1)} %bitcast.212), kind=kLoop, calls=%fused_computation.49 | loop fusion | flops 2881536 | bytes 65536 | tf_op jit(solution)/shard_map/while/body/eval_jaxpr/vmap()/reduce_sum | solution.py:43
  126.9 1.3 multiply_reduce_fusion.1
  128.2 2.6 %multiply_reduce_fusion = (f32[16,128]{1,0:T(8,128)S(1)}, f32[16,128]{1,0:T(8,128)S(1)}, f32[16,128]{1,0:T(8,128)S(1)}, f32[16,128]{1,0:T(8,128)S(1)}) fusion(f32[16,128]{1,0:T(8,128)S(1)} %broadcast_add_fusion, f32[16,128]{1,0:T(8,128)S(1)} %bitcast.215, f32[16,128]{1,0:T(8,128)S(1)} %bitcast.205, f32[16,128]{1,0:T(8,128)S(1)} %bitcast.217, ...), kind=kLoop, calls=%fused_computation.47 | loop fusion | flops 6545408 | bytes 131072 | tf_op jit(solution)/shard_map/while/body/eval_jaxpr/vmap()/reduce_sum | solution.py:45
  131.0 0.7 bitcast_select_fusion
  (123 shorter events, 6.3 us)
Async XLA Ops:
  0.6 2.6 %copy-start = (f32[3,4096]{1,0:T(4,128)S(1)}, f32[3,4096]{1,0:T(4,128)}, u32[]{:S(2)}) copy-start(f32[3,4096]{1,0:T(4,128)} %param.21) | copy-start | bytes 147460
  3.3 9.5 %copy-start.6 = (s32[16,1]{0,1:T(1,128)S(1)}, s32[16,1]{0,1:T(1,128)}, u32[]{:S(2)}) copy-start(s32[16,1]{0,1:T(1,128)} %param.30) | copy-start | bytes 196
  3.3 9.7 %copy-start.8 = (s32[16]{0:T(128)S(1)}, s32[16]{0:T(128)}, u32[]{:S(2)}) copy-start(s32[16]{0:T(128)} %param.31) | copy-start | bytes 196
  3.3 9.8 %copy-start.7 = (s32[16]{0:T(128)S(1)}, s32[16]{0:T(128)}, u32[]{:S(2)}) copy-start(s32[16]{0:T(128)} %param.29) | copy-start | bytes 196
  3.4 9.9 %copy-start.4 = (f32[2048]{0:T(1024)S(1)}, f32[2048]{0:T(1024)}, u32[]{:S(2)}) copy-start(f32[2048]{0:T(1024)} %param.27) | copy-start | bytes 24580
  3.4 9.9 %copy-start.2 = (f32[3,2048]{1,0:T(4,128)S(1)}, f32[3,2048]{1,0:T(4,128)}, u32[]{:S(2)}) copy-start(f32[3,2048]{1,0:T(4,128)} %param.28) | copy-start | bytes 73732
  3.9 15.0 %collective-permute-start = (f32[4,256]{1,0:T(4,128)S(1)}, f32[4,256]{1,0:T(4,128)S(1)}, u32[]{:S(2)}, u32[]{:S(2)}) collective-permute-start(f32[4,256]{1,0:T(4,128)S(1)} %bitcast.236), channel_id=1, source_target_pairs={{0,8},{8,16},{16,24},{24,0},{1,9},{9,17},{17,25},{25,1},{2,10},{10... | collective-permute-start | bytes 12296 | tf_op jit(solution)/shard_map/ppermute | solution.py:20
  7.0 6.3 %copy-start.3 = (f32[3,2048]{1,0:T(4,128)S(1)}, f32[3,2048]{1,0:T(4,128)}, u32[]{:S(2)}) copy-start(f32[3,2048]{1,0:T(4,128)} %param.26) | copy-start | bytes 73732
  7.6 11.4 %collective-permute-start.1 = (f32[4,256]{1,0:T(4,128)S(1)}, f32[4,256]{1,0:T(4,128)S(1)}, u32[]{:S(2)}, u32[]{:S(2)}) collective-permute-start(f32[4,256]{1,0:T(4,128)S(1)} %bitcast.234), channel_id=1, source_target_pairs={{0,24},{8,0},{16,8},{24,16},{1,25},{9,1},{17,9},{25,17},{2,26},{10... | collective-permute-start | bytes 12296 | tf_op jit(solution)/shard_map/ppermute | solution.py:20
  10.3 8.7 %collective-permute-start.2 = (f32[4,256]{1,0:T(4,128)S(1)}, f32[4,256]{1,0:T(4,128)S(1)}, u32[]{:S(2)}, u32[]{:S(2)}) collective-permute-start(f32[4,256]{1,0:T(4,128)S(1)} %bitcast.237), channel_id=1, source_target_pairs={{0,2},{2,4},{4,6},{6,0},{1,3},{3,5},{5,7},{7,1},{8,10},{10,12},{12... | collective-permute-start | bytes 12296 | tf_op jit(solution)/shard_map/ppermute | solution.py:20
  10.9 8.2 %collective-permute-start.3 = (f32[4,256]{1,0:T(4,128)S(1)}, f32[4,256]{1,0:T(4,128)S(1)}, u32[]{:S(2)}, u32[]{:S(2)}) collective-permute-start(f32[4,256]{1,0:T(4,128)S(1)} %bitcast.235), channel_id=1, source_target_pairs={{0,6},{2,0},{4,2},{6,4},{1,7},{3,1},{5,3},{7,5},{8,14},{10,8},{12,... | collective-permute-start | bytes 12296 | tf_op jit(solution)/shard_map/ppermute | solution.py:20
  14.3 109.6 %all-to-all-start = ((f32[8,3,8,128]{3,2,1,0:T(8,128)}), f32[8,3,8,128]{3,2,1,0:T(8,128)S(1)}, u32[]{:S(2)}, u32[]{:S(2)}) async-start(f32[8,3,8,128]{3,2,1,0:T(8,128)} %copy.32), calls=%async_computation | async-start | bytes 196608 | tf_op jit(solution)/shard_map/all_to_all | solution.py:152
  18.2 0.7 copy-start.5
  124.1 0.6 copy-start.1
  124.7 0.8 slice-start
where the time goes:
time: 132 us
  other arithmetic  112 us (85%)
  starting transfers between devices  10.9 us (8%)
  local copies, waits for them, and re-layouts  6.74 us (5%)
    reduce_sum x16, other arithmetic, pair_accel(): jnp.sum(sep_x * kernel, axis=1)  102 us
    ppermute x4, starting transfers between devices, from_behind(): lax.ppermute(shard, axis, [(i, (i + by) % size) for i in range(size)])  7.01 us
    all_to_all x1, starting transfers between devices, on_device(): lax.all_to_all(outgoing, ('gy', 'gz'), split_axis=0, concat_axis=0, tiled...  3.91 us
    reduce_sum x2, other arithmetic, deposit_block(): heated = jnp.sum(energy_in[:, None] * shares, axis=0)  3.84 us
  transfers between devices with their start and end apart: 5, of which 0 were waited for; matrix products, arithmetic and copies ran while one was open for 82% of the time, Pallas kernels for 0%

commit v1 on v0

v1 whole, which is shorter than its diff:
```python
import functools
import math

import jax
import jax.numpy as jnp
from jax import lax
from jax.experimental import pallas as pl
from jax.experimental.pallas import tpu as pltpu
from jax.sharding import PartitionSpec as P

LANES = 128
SLOTS = 3
SPLIT_SQ = 1.0
SOFT_SQ = 0.01
GRAVITY = 0.002
RADIAL_PUSH = 1.0

SCALE = math.log2(math.e) / (1.5 * SPLIT_SQ)
FACTOR = GRAVITY * math.exp(SOFT_SQ / SPLIT_SQ) * SCALE**1.5
FEATURES = 40
MESH = pl.DeviceIdType.MESH
HIGHEST = lax.Precision.HIGHEST
F32 = jnp.float32
BF16 = jnp.bfloat16

TARGETS = 512
SOURCES = 256
UNROLL = 4


def split3(x):
    a = x.astype(BF16).astype(F32)
    rest = x - a
    b = rest.astype(BF16).astype(F32)
    return a, b, rest - b


def prepare_sends(
    sizes,
    pos_ref, mass_ref, count_ref, ghost_ref,
    star_pos_ref, energy_ref, star_mom_ref, block_count_ref, owner_ref, leaf_ref,
    src, ghost_send, star_send,
):
    n_x, n_y, n_z, leaves, ghosts, blocks = sizes
    owners = n_y * n_z
    rows = leaves * LANES
    lane = lax.broadcasted_iota(jnp.int32, (1, LANES), 1)

    src[0:3, :] = pos_ref[...]
    src[4:8, :] = jnp.zeros((4, rows), F32)
    for l in range(leaves):
        here = slice(l * LANES, (l + 1) * LANES)
        alive = lane < count_ref[l]
        src[3:4, here] = jnp.where(alive, mass_ref[l : l + 1, :], 0.0)
        src[4:5, here] = jnp.where(alive, 1.0, 0.0).astype(F32)
    for k in range(4):
        for g in range(ghosts):
            start = pl.multiple_of(ghost_ref[k * ghosts + g] * LANES, LANES)
            ghost_send[k, :, g * LANES : (g + 1) * LANES] = src[:, pl.ds(start, LANES)]

    @pl.loop(0, owners)
    def _(o):
        def scan(b, found):
            hit = owner_ref[b] == o
            i0, i1, i2 = found
            return (jnp.where(hit, b, i0), jnp.where(hit, i0, i1), jnp.where(hit, i1, i2))

        none = jnp.int32(-1)
        found = lax.fori_loop(0, blocks, scan, (none,) * SLOTS, unroll=8)
        for k in range(SLOTS):
            b = jnp.maximum(found[k], 0)
            valid = found[k] >= 0
            start = pl.multiple_of(b * LANES, LANES)
            live = lane < jnp.where(valid, block_count_ref[b], 0)
            named = lane == jnp.where(valid, leaf_ref[b], -1)
            star_send[o, k, 0:3] = star_pos_ref[:, pl.ds(start, LANES)]
            star_send[o, k, 3:4] = jnp.where(live, energy_ref[pl.ds(b, 1), :], 0.0)
            star_send[o, k, 4:7] = jnp.where(live, star_mom_ref[:, pl.ds(start, LANES)], 0.0)
            star_send[o, k, 7:8] = jnp.where(named, 1.0, 0.0).astype(F32)


def kernel(
    sizes,
    own_ref, smooth_ref, ghost_send, star_send,
    accel_ref, deposit_ref,
    src, ghost_recv, star_recv,
    feat, side_a, side_b, weights, acc, table, marker, gathered, dep,
    ghost_ssem, ghost_rsem, star_ssem, star_rsem,
):
    n_x, n_y, n_z, leaves, ghosts, blocks = sizes
    owners = n_y * n_z
    rows = leaves * LANES
    wide = ghosts * LANES
    x, y, z = lax.axis_index("gx"), lax.axis_index("gy"), lax.axis_index("gz")
    me = y * n_z + z

    def owner_at(d):
        other = lax.rem(me + d, owners)
        return other, (x, lax.div(other, n_z), lax.rem(other, n_z))

    def beside(k):
        step = 1 if k % 2 == 0 else -1
        if k < 2:
            return (lax.rem(x + step + n_x, n_x), y, z)
        return (x, lax.rem(y + step + n_y, n_y), z)

    barrier = pltpu.get_barrier_semaphore()
    for k in range(2):
        pl.semaphore_signal(barrier, inc=1, device_id=beside(k), device_id_type=MESH)

    @pl.loop(1, owners)
    def _(d):
        pl.semaphore_signal(barrier, inc=1, device_id=owner_at(d)[1], device_id_type=MESH)

    src[:, 0:rows] = own_ref[...]
    pl.semaphore_wait(barrier, owners + 1)

    def ghost_copy(k):
        return pltpu.make_async_remote_copy(
            src_ref=ghost_send.at[k], dst_ref=ghost_recv.at[k],
            send_sem=ghost_ssem.at[k], recv_sem=ghost_rsem.at[k],
            device_id=beside(k), device_id_type=MESH,
        )

    def star_copy(d):
        other, where = owner_at(d)
        return pltpu.make_async_remote_copy(
            src_ref=star_send.at[other], dst_ref=star_recv.at[me],
            send_sem=star_ssem.at[d], recv_sem=star_rsem.at[d],
            device_id=where, device_id_type=MESH,
        )

    for k in range(4):
        ghost_copy(k).start()

    @pl.loop(1, owners)
    def _(d):
        star_copy(d).start()

    star_recv[me] = star_send[me]

    def put(rows_of):
        at = 0
        for piece in rows_of:
            feat[at : at + piece.shape[0], :] = piece
            at += piece.shape[0]
        if at < FEATURES:
            feat[at:FEATURES, :] = jnp.zeros((FEATURES - at, SOURCES), F32)

    def prepare(start, targets):
        here = pl.ds(start, SOURCES)
        u = src[0:3, here] - 0.5
        mass = src[3:4, here]
        norm = SCALE * jnp.sum(u * u, axis=0, keepdims=True)
        a = split3((-2.0 * SCALE) * u)
        n = split3(norm + SCALE * SOFT_SQ)
        one = jnp.ones((1, SOURCES), F32)
        put([a[0]] * 3 + [a[1]] * 3 + [a[2]] * 3 + list(n) + [one] * 3)
        side_a[here, :] = feat[...].T.astype(BF16)
        wx, wm = split3(mass * u), split3(mass)
        put([wx[0], wm[0], wx[1], wm[1], wx[2], wm[2]])
        weights[:, here] = feat[0:16, :].astype(BF16)
        if targets:
            b = split3(u)
            put(list(b) * 3 + [one] * 3 + list(split3(norm)))
            side_b[:, here] = feat[...].astype(BF16)

    @pl.loop(0, rows // SOURCES)
    def _(c):
        prepare(pl.multiple_of(c * SOURCES, SOURCES), True)

    def pairs(start, right):
        d = jnp.dot(
            side_a[pl.ds(start, SOURCES), :], right, preferred_element_type=F32
        )
        value = jnp.exp2(-1.5 * (d + lax.log2(d)))
        high = value.astype(BF16)
        low = (value - high.astype(F32)).astype(BF16)
        w = weights[:, pl.ds(start, SOURCES)]
        return jnp.dot(w, high, preferred_element_type=F32) + jnp.dot(
            w, low, preferred_element_type=F32
        )

    def over(first, count, right, total, unroll):
        def step(c, total):
            start = pl.multiple_of(first + c * SOURCES, SOURCES)
            return total + pairs(start, right)

        return lax.fori_loop(0, count, step, total, unroll=unroll)

    @pl.loop(0, rows // TARGETS)
    def _(t):
        here = pl.ds(pl.multiple_of(t * TARGETS, TARGETS), TARGETS)
        acc[:, here] = over(
            0, rows // SOURCES, side_b[:, here], jnp.zeros((16, TARGETS), F32), UNROLL
        )

    for k in range(4):
        ghost_copy(k).wait()
        there = slice(rows + k * wide, rows + (k + 1) * wide)
        src[:, there] = ghost_recv[k]
        shifted = slice(k // 2, k // 2 + 1)
        src[shifted, there] = src[shifted, there] + (-1.0 if k % 2 == 0 else 1.0)

    @pl.loop(0, 4 * wide // SOURCES)
    def _(c):
        prepare(pl.multiple_of(rows + c * SOURCES, SOURCES), False)

    @pl.loop(0, rows // TARGETS)
    def _(t):
        here = pl.ds(pl.multiple_of(t * TARGETS, TARGETS), TARGETS)
        total = over(rows, 4 * wide // SOURCES, side_b[:, here], acc[:, here], True)
        total = total[0:4] + total[4:8] + total[8:12]
        u = src[0:3, here] - 0.5
        value = FACTOR * (total[0:3] - u * total[3:4])
        accel_ref[:, here] = jnp.where(src[4:5, here] > 0.5, value, 0.0)

    h = smooth_ref[...]
    table[:, 3 * LANES :] = 1.0 / (h * h)
    for l in range(leaves):
        for c in range(3):
            table[l : l + 1, c * LANES : (c + 1) * LANES] = src[
                c : c + 1, l * LANES : (l + 1) * LANES
            ]

    @pl.loop(1, owners)
    def _(d):
        star_copy(d).wait()

    @pl.loop(0, owners)
    def _(o):
        for k in range(SLOTS):
            marker[pl.ds(o * SLOTS + k, 1), :] = star_recv[o, k, 7:8]

    for c in range(4):
        gathered[c] = jnp.dot(
            marker[:, 0:leaves],
            table[:, c * LANES : (c + 1) * LANES],
            precision=HIGHEST,
            preferred_element_type=F32,
        )

    @pl.loop(0, owners)
    def _(o):
        for k in range(SLOTS):
            at = pl.ds(o * SLOTS + k, 1)
            star = star_recv[o, k].T
            gas = [gathered[c, at, :] for c in range(4)]
            seps = [gas[c] - star[:, c : c + 1] for c in range(3)]
            distance = seps[0] * seps[0] + seps[1] * seps[1] + seps[2] * seps[2]
            weight = jnp.exp(-distance * gas[3])
            share = weight / (1.0 + jnp.sum(weight, axis=1, keepdims=True))
            heat = star[:, 3:4] * share
            dep[0, at, :] = jnp.sum(heat, axis=0, keepdims=True)
            for c in range(3):
                kick = share * star[:, 4 + c : 5 + c] + RADIAL_PUSH * heat * seps[c]
                dep[c + 1, at, :] = jnp.sum(kick, axis=0, keepdims=True)

    named = marker[...].T[0:leaves]
    for c in range(4):
        table[:, c * LANES : (c + 1) * LANES] = jnp.dot(
            named, dep[c], precision=HIGHEST, preferred_element_type=F32
        )
    for l in range(leaves):
        alive = src[4:5, l * LANES : (l + 1) * LANES] > 0.5
        for c in range(4):
            deposit_ref[c : c + 1, l * LANES : (l + 1) * LANES] = jnp.where(
                alive, table[l : l + 1, c * LANES : (c + 1) * LANES], 0.0
            )


def on_device(
    mesh_sizes,
    gas_position, gas_mass, gas_smoothing, leaf_counts, ghost_lists,
    star_position, star_energy, star_momentum, block_counts, block_owners, block_leaves,
):
    n_x, n_y, n_z = mesh_sizes
    leaves = leaf_counts.shape[0]
    blocks = block_counts.shape[0]
    ghosts = ghost_lists.shape[2]
    rows = leaves * LANES
    owners = n_y * n_z
    slots = owners * SLOTS
    slot_rows = -(-slots // 8) * 8
    total = rows + 4 * ghosts * LANES
    vmem = pl.BlockSpec(memory_space=pltpu.VMEM)
    smem = pl.BlockSpec(memory_space=pltpu.SMEM)
    sizes = (n_x, n_y, n_z, leaves, ghosts, blocks)
    own, ghost_send, star_send = pl.pallas_call(
        functools.partial(prepare_sends, sizes),
        out_shape=(
            jax.ShapeDtypeStruct((8, rows), F32),
            jax.ShapeDtypeStruct((4, 8, ghosts * LANES), F32),
            jax.ShapeDtypeStruct((owners, SLOTS, 8, LANES), F32),
        ),
        in_specs=[vmem, vmem, smem, smem, vmem, vmem, vmem, smem, smem, smem],
        out_specs=(vmem, vmem, vmem),
    )(
        gas_position,
        gas_mass.reshape(leaves, LANES),
        leaf_counts,
        ghost_lists.reshape(-1),
        star_position,
        star_energy.reshape(blocks, LANES),
        star_momentum,
        block_counts,
        block_owners.reshape(-1),
        block_leaves,
    )
    return pl.pallas_call(
        functools.partial(kernel, sizes),
        out_shape=(
            jax.ShapeDtypeStruct((3, rows), F32),
            jax.ShapeDtypeStruct((4, rows), F32),
        ),
        in_specs=[vmem, vmem, vmem, vmem],
        out_specs=(vmem, vmem),
        scratch_shapes=[
            pltpu.VMEM((8, total), F32),
            pltpu.VMEM((4, 8, ghosts * LANES), F32),
            pltpu.VMEM((owners, SLOTS, 8, LANES), F32),
            pltpu.VMEM((FEATURES, SOURCES), F32),
            pltpu.VMEM((total, FEATURES), BF16),
            pltpu.VMEM((FEATURES, rows), BF16),
            pltpu.VMEM((16, total), BF16),
            pltpu.VMEM((16, rows), F32),
            pltpu.VMEM((leaves, 4 * LANES), F32),
            pltpu.VMEM((slot_rows, LANES), F32),
            pltpu.VMEM((4, slot_rows, LANES), F32),
            pltpu.VMEM((4, slot_rows, LANES), F32),
            pltpu.SemaphoreType.DMA((4,)),
            pltpu.SemaphoreType.DMA((4,)),
            pltpu.SemaphoreType.DMA((owners,)),
            pltpu.SemaphoreType.DMA((owners,)),
        ],
        compiler_params=pltpu.CompilerParams(collective_id=0, has_side_effects=True),
    )(own, gas_smoothing.reshape(leaves, LANES), ghost_send, star_send)


def solution(mesh):
    split = ("gx", "gy", "gz")
    placed = (
        P(None, split), P(split), P(split), P(split), P(split, None, None),
        P(None, split), P(split), P(None, split), P(split), P(split, None), P(split),
    )
    sizes = tuple(mesh.shape[axis] for axis in split)
    return jax.shard_map(
        functools.partial(on_device, sizes),
        mesh=mesh,
        in_specs=placed,
        out_specs=(P(None, split), P(None, split)),
        check_vma=False,
    )
```

time: 132 us -> 80.5 us (0.61)
  other arithmetic: 112 us -> 0 us
  Pallas kernels: 0 us -> 76.1 us
  starting transfers between devices: 10.9 us -> 0 us
  local copies, waits for them, and re-layouts: 6.74 us -> 3.51 us
    reduce_sum x21 -> x0, other arithmetic: 108 us -> none  [the longest x16 102 us: pair_accel(): jnp.sum(sep_x * kernel, axis=1)]
    pallas_call x0 -> x2, Pallas kernels: none -> 76.1 us  [the longest x1 74.1 us: on_device(): pl.pallas_call(functools.partial(kernel, sizes), out_shape=(jax.ShapeDtyp...]
    ppermute x4 -> x0, starting transfers between devices: 7.01 us -> none  [from_behind(): lax.ppermute(shard, axis, [(i, (i + by) % size) for i in range(size)])]
    all_to_all x1 -> x0, starting transfers between devices: 3.91 us -> none  [on_device(): lax.all_to_all(outgoing, ('gy', 'gz'), split_axis=0, concat_axis=0, tiled...]
    slice x40 -> x0, local copies, waits for them, and re-layouts: 2.39 us -> none  [the longest x1 1.04 us: gather_ghosts(): outbound = carried[:, leaf_lists[which], :].reshape(4, -1)]
    gather x4 -> x0, local copies, waits for them, and re-layouts: 2.28 us -> none  [gather_ghosts(): outbound = carried[:, leaf_lists[which], :].reshape(4, -1)]
    select_n x7 -> x0, other arithmetic: 2.24 us -> none  [the longest x1 0.79 us: on_device(): masses = jnp.where(alive, gas_mass, jnp.float32(0.0))]
    unnamed x21 -> x7, local copies, waits for them, and re-layouts: 1.24 us -> 2.91 us
  transfers between devices with their start and end apart: 5 -> 0, of which waited for: 0 -> 0; matrix products, arithmetic and copies ran while one was open for 82% -> 0% of each run, Pallas kernels for 0% -> 0%
where the time goes in v1:
time: 80.5 us; the launch traced here: 80.3 us
  Pallas kernels  76.1 us (95%)
  local copies, waits for them, and re-layouts  3.51 us (4%)
    pallas_call x1, Pallas kernels, on_device(): pl.pallas_call(functools.partial(kernel, sizes), out_shape=(jax.ShapeDtyp...  74.1 us
    unnamed x7, local copies, waits for them, and re-layouts  2.91 us
    pallas_call x1, Pallas kernels, on_device(): pl.pallas_call(functools.partial(prepare_sends, sizes), out_shape=(jax.Sh...  2.03 us

profile of v1, /device:TPU:0, one launch (start us, length us, event | category | flops | bytes accessed | tf_op | source)
XLA Modules:
  0.0 80.3 jit_solution(6730849126319539477)
XLA Ops:
  0.6 0.0 copy-start.1
  0.6 0.7 copy-done.1
  1.3 0.1 copy.14
  1.4 0.6 reshape.20.ghost_ref
  2.0 2.0 %shard_map.122 = (f32[8,4096]{1,0:T(8,128)}, f32[4,8,256]{2,1,0:T(8,128)}, f32[8,3,8,128]{3,2,1,0:T(8,128)}) custom-call(f32[3,4096]{1,0:T(4,128)} %pos_ref.1, f32[32,128]{1,0:T(8,128)} %bitcast.4, s32[32]{0:T(128)} %count_ref.1, s32[8]{0:T(128)} %reshape.20.ghost_ref, f32[3,2048]{1,0:T(4,128)} %star_pos_ref.1, f32[16,128]{1,0:T(8,128)} %bitcast.6, ...), custom_call_target="tpu_custom_call" | custom-call | tf_op jit(solution)/shard_map/pallas_call | solution.py:289
  4.0 74.1 %shard_map.123 = (f32[3,4096]{1,0:T(4,128)}, f32[4,4096]{1,0:T(4,128)}) custom-call(f32[8,4096]{1,0:T(8,128)} %get-tuple-element.5.own_ref, f32[32,128]{1,0:T(8,128)} %bitcast.5, f32[4,8,256]{2,1,0:T(8,128)} %get-tuple-element.6.ghost_send, f32[8,3,8,128]{3,2,1,0:T(8,128)} %get-tuple-element.7.star_send), custom_call_target="tpu_custom_call" | custom-call | tf_op jit(solution)/shard_map/pallas_call | solution.py:310
  78.1 0.0 copy-start
  78.1 1.5 %copy.17 = f32[3,4096]{1,0:T(4,128)} copy(f32[3,4096]{1,0:T(4,128)} %get-tuple-element.10) | data formatting | bytes 98304
  79.7 0.0 copy-done
  79.7 0.6 copy.18
Async XLA Ops:
  0.6 0.7 copy-start.1
  78.1 1.5 %copy-start = (f32[4,4096]{1,0:T(4,128)S(1)}, f32[4,4096]{1,0:T(4,128)}, u32[]{:S(2)}) copy-start(f32[4,4096]{1,0:T(4,128)} %get-tuple-element.11) | copy-start | bytes 196612

commit v2 on v1

--- a/solution.py
+++ b/solution.py
@@ -23,9 +23,9 @@
 F32 = jnp.float32
 BF16 = jnp.bfloat16
 
-TARGETS = 512
+TARGETS = 1024
 SOURCES = 256
-UNROLL = 4
+UNROLL = 2
 
 
 def split3(x):

time: 80.5 us -> 68.6 us (0.85)
  Pallas kernels: 76.1 us -> 64.2 us
    pallas_call x1, Pallas kernels: 74.1 us -> 62.1 us  [on_device(): pl.pallas_call(functools.partial(kernel, sizes), out_shape=(jax.ShapeDtyp...]
where the time goes in v2:
time: 68.6 us; the launch traced here: 68.3 us
  Pallas kernels  64.2 us (94%)
  local copies, waits for them, and re-layouts  3.51 us (5%)
    pallas_call x1, Pallas kernels, on_device(): pl.pallas_call(functools.partial(kernel, sizes), out_shape=(jax.ShapeDtyp...  62.1 us
    unnamed x7, local copies, waits for them, and re-layouts  2.91 us
    pallas_call x1, Pallas kernels, on_device(): pl.pallas_call(functools.partial(prepare_sends, sizes), out_shape=(jax.Sh...  2.03 us

profile of v2, /device:TPU:0, one launch (start us, length us, event | category | flops | bytes accessed | tf_op | source)
XLA Modules:
  0.0 68.3 jit_solution(17068169215415798605)
XLA Ops:
  0.6 0.0 copy-start.1
  0.6 0.7 copy-done.1
  1.3 0.1 copy.14
  1.4 0.6 reshape.20.ghost_ref
  2.0 2.0 %shard_map.122 = (f32[8,4096]{1,0:T(8,128)}, f32[4,8,256]{2,1,0:T(8,128)}, f32[8,3,8,128]{3,2,1,0:T(8,128)}) custom-call(f32[3,4096]{1,0:T(4,128)} %pos_ref.1, f32[32,128]{1,0:T(8,128)} %bitcast.4, s32[32]{0:T(128)} %count_ref.1, s32[8]{0:T(128)} %reshape.20.ghost_ref, f32[3,2048]{1,0:T(4,128)} %star_pos_ref.1, f32[16,128]{1,0:T(8,128)} %bitcast.6, ...), custom_call_target="tpu_custom_call" | custom-call | tf_op jit(solution)/shard_map/pallas_call | solution.py:289
  4.0 62.1 %shard_map.123 = (f32[3,4096]{1,0:T(4,128)}, f32[4,4096]{1,0:T(4,128)}) custom-call(f32[8,4096]{1,0:T(8,128)} %get-tuple-element.5.own_ref, f32[32,128]{1,0:T(8,128)} %bitcast.5, f32[4,8,256]{2,1,0:T(8,128)} %get-tuple-element.6.ghost_send, f32[8,3,8,128]{3,2,1,0:T(8,128)} %get-tuple-element.7.star_send), custom_call_target="tpu_custom_call" | custom-call | tf_op jit(solution)/shard_map/pallas_call | solution.py:310
  66.2 0.0 copy-start
  66.2 1.5 %copy.17 = f32[3,4096]{1,0:T(4,128)} copy(f32[3,4096]{1,0:T(4,128)} %get-tuple-element.10) | data formatting | bytes 98304
  67.7 0.0 copy-done
  67.7 0.6 copy.18
Async XLA Ops:
  0.6 0.7 copy-start.1
  66.2 1.5 %copy-start = (f32[4,4096]{1,0:T(4,128)S(1)}, f32[4,4096]{1,0:T(4,128)}, u32[]{:S(2)}) copy-start(f32[4,4096]{1,0:T(4,128)} %get-tuple-element.11) | copy-start | bytes 196612
